TPU v7x, 256 devices: a whole 4x4x8 slice. The times are simulated.
256 devices in a mesh: wide: 64 (over z, y, core), narrow: 4 (over x).
Axes of the slice: x: 4, y: 4, z: 8, core: 2. Of those that a mesh axis runs over, the one named last changes fastest.
Arguments:
- coords_inner: float32 [2, 65536], P(None, ('wide', 'narrow')), may hold values from -1 to 1
- velocity: float32 [2, 65536], P(None, ('wide', 'narrow')), may hold values from -6 to 6
- source: float32 [65536], P(('wide', 'narrow')), may hold values from -6 to 6
- coords_edge: float32 [2, 32768], P(None, ('wide', 'narrow')), may hold values from -1 to 1
- flux_weight: float32 [2, 32768], P(None, ('wide', 'narrow')), may hold values from -6 to 6
- owner: int32 [32768, 1], P(('wide', 'narrow')), may hold values from 0 to 63; in each aligned block of 128 rows (0 to 127, 128 to 255, ...) at most 4 rows name the same one
- local_face: int32 [32768], P(('wide', 'narrow')), may hold values from 0 to 127
- w_first: float32 [2, 512], replicated, may hold values from -4 to 4
- b_first: float32 [512], replicated, may hold values from -3 to 3
- w_hidden: float32 [4, 512, 512], replicated, may hold values from -0.25 to 0.25
- b_hidden: float32 [4, 512], replicated, may hold values from -3 to 3
- w_last: float32 [512], replicated, may hold values from -0.25 to 0.25
Outputs:
- face_integral: float32 [8192], P('wide')
- grad_first: float32 [2, 512], replicated
- grad_hidden: float32 [4, 512, 512], replicated
- grad_last: float32 [512], replicated
Inputs may be any that keep to these rules, and one draw needn't show every extreme that they name: Among the 128 face points of one device no owner appears more than 4 times, and some owner appears exactly 4 times.
All inputs are finite; a program needn't handle non-finite values.
Results may differ from a plain program's by a relative error of at most 0.0003.
Values sent between devices are 32-bit elements; how exact they have to be, the bound alone decides.
A program may use at most 128 MiB of HBM per device.

v0:
```python
import math
import jax
import jax.numpy as jnp
from jax import lax
from jax.sharding import PartitionSpec as P

FACE_DEV = 128
penalty_weight = 4.0
BOTH = ("wide", "narrow")
precise = lax.Precision.HIGH


def forward(coords, direction, w_first, b_first, w_hidden, b_hidden, w_last):
    hidden = jnp.tanh(
        coords[0][:, None] * w_first[0][None] + coords[1][:, None] * w_first[1][None] + b_first
    )
    tangent = (1.0 - hidden * hidden) * (
        direction[0][:, None] * w_first[0][None] + direction[1][:, None] * w_first[1][None]
    )
    points = hidden.shape[0]
    kept = [(hidden, None, tangent)]
    for level in range(w_hidden.shape[0]):
        product = jnp.dot(jnp.concatenate([hidden, tangent], 0), w_hidden[level], precision=precise)
        hidden = jnp.tanh(product[:points] + b_hidden[level])
        slope = product[points:]
        tangent = (1.0 - hidden * hidden) * slope
        kept.append((hidden, slope, tangent))
    value = jnp.sum(hidden * w_last[None], 1)
    slopes = jnp.sum(tangent * w_last[None], 1)
    return (value, slopes, kept)


def backward(coords, direction, kept, hidden_cot, tangent_cot, w_first, w_hidden):
    grads = []
    for level in reversed(range(w_hidden.shape[0])):
        hidden, slope, _ = kept[level + 1]
        gate = 1.0 - hidden * hidden
        product_cot = gate * tangent_cot
        sum_cot = gate * (hidden_cot - 2.0 * hidden * slope * tangent_cot)
        cots = jnp.concatenate([sum_cot, product_cot], 0)
        below = jnp.concatenate([kept[level][0], kept[level][2]], 0)
        grads.append(lax.dot_general(below, cots, (((0,), (0,)), ((), ())), precision=precise))
        down = lax.dot_general(cots, w_hidden[level], (((1,), (1,)), ((), ())), precision=precise)
        points = hidden.shape[0]
        hidden_cot, tangent_cot = (down[:points], down[points:])
    hidden, _, _ = kept[0]
    gate = 1.0 - hidden * hidden
    start = direction[0][:, None] * w_first[0][None] + direction[1][:, None] * w_first[1][None]
    start_cot = gate * tangent_cot
    sum_cot = gate * (hidden_cot - 2.0 * hidden * start * tangent_cot)
    first = jnp.stack(
        [
            jnp.sum(coords[j][:, None] * sum_cot + direction[j][:, None] * start_cot, 0)
            for j in range(2)
        ]
    )
    return (first, jnp.stack(grads[::-1], 0))


def local(
    coords_inner,
    velocity,
    source,
    coords_edge,
    flux_weight,
    owner,
    local_face,
    w_first,
    b_first,
    w_hidden,
    b_hidden,
    w_last,
):
    devices = lax.axis_size(BOTH)
    inner_rows = coords_inner.shape[1]
    edge_rows = coords_edge.shape[1]
    inner_scale = 2.0 / math.sqrt(inner_rows * devices)
    face_scale = 2.0 * penalty_weight / math.sqrt(FACE_DEV * lax.axis_size("wide"))
    net = (w_first, b_first, w_hidden, b_hidden, w_last)
    _, flux, kept_edge = forward(coords_edge, flux_weight, *net)
    face = owner[:, 0] * FACE_DEV + local_face
    mine = jnp.stack([flux, face.astype(jnp.float32)], 0)
    everyone = lax.all_gather(mine, BOTH)
    all_flux = everyone[:, 0].reshape(-1)
    all_face = everyone[:, 1].reshape(-1)

    def sums(wanted):
        return jnp.sum(
            jnp.where(wanted.astype(jnp.float32)[:, None] == all_face[None], all_flux[None], 0.0), 1
        )

    reached = sums(face)
    integral = sums(lax.axis_index("wide") * FACE_DEV + jnp.arange(FACE_DEV))
    value, slopes, kept_inner = forward(coords_inner, velocity, *net)
    inner_cot = inner_scale * (slopes + value - source)
    edge_cot = face_scale * reached
    coords = jnp.concatenate([coords_inner, coords_edge], 1)
    direction = jnp.concatenate([velocity, flux_weight], 1)
    kept = [
        tuple((None if a is None else jnp.concatenate([a, b], 0) for a, b in zip(one, two)))
        for one, two in zip(kept_inner, kept_edge)
    ]
    hidden_out = jnp.concatenate([inner_cot, jnp.zeros_like(edge_cot)])[:, None]
    tangent_out = jnp.concatenate([inner_cot, edge_cot])[:, None]
    last = jnp.sum(hidden_out * kept[-1][0] + tangent_out * kept[-1][2], 0)
    first, hidden = backward(
        coords,
        direction,
        kept,
        hidden_out * w_last[None],
        tangent_out * w_last[None],
        w_first,
        w_hidden,
    )
    first, hidden, last = lax.psum((first, hidden, last), BOTH)
    return (integral, first, hidden, last)


def solution(mesh):
    points = P(None, BOTH)
    in_specs = (
        points,
        points,
        P(BOTH),
        points,
        points,
        P(BOTH, None),
        P(BOTH),
        P(),
        P(),
        P(),
        P(),
        P(),
    )
    out_specs = (P("wide"), P(), P(), P())
    return jax.shard_map(local, mesh=mesh, in_specs=in_specs, out_specs=out_specs, check_vma=False)
```

profile of v0, /device:TPU:2, one launch (start us, length us, event | category | flops | bytes accessed | tf_op | source)
XLA Modules:
  0.0 388.6 jit_solution(4115349576246029402)
XLA Ops:
  7.2 0.0 all-reduce.4.cloned.1.call-start
  7.2 0.8 fusion.155
  8.0 0.8 fusion.156
  8.7 0.8 fusion.154
  9.5 0.9 fusion.153
  10.4 0.8 slice_bitcast_fusion.1
  11.1 0.8 add_tanh_fusion.1
  12.0 1.8 fusion.78
  13.8 0.0 copy-start
  13.8 0.1 subtract_multiply_fusion.7
  13.9 2.0 fusion.74
  15.9 0.1 subtract_multiply_fusion.6
  16.0 0.3 copy-done
  16.3 0.7 fusion.70
  17.0 0.0 copy-start.8
  17.0 0.0 copy-start.9
  17.0 0.0 copy-start.1
  17.0 0.1 subtract_multiply_fusion.5
  17.1 0.6 fusion.66
  17.8 0.0 copy-done.8
  17.8 0.0 copy-done.9
  17.8 0.0 copy-start.2
  17.8 0.0 copy-done.1
  17.8 0.2 multiply_reduce_fusion.2
  18.0 67.6 %all-gather.1 = f32[256,2,128]{2,1,0:T(2,128)S(1)} all-gather(f32[1,2,128]{2,1,0:T(2,128)S(1)} %maximum_bitcast_fusion), channel_id=2, replica_groups=mesh['wide'=64,'narrow'=4] {'wide','narrow'}, dimensions={0}, use_global_device_ids=true | all-gather | bytes 263168 | tf_op jit(solution)/shard_map/all_gather | solution.py:83
  85.6 0.2 fusion.152
  85.8 4.7 %select_reduce_fusion = (f32[128]{0:T(128)S(1)}, f32[128]{0:T(128)}) fusion(f32[32768]{0:T(1024)S(1)} %bitcast.67, f32[32768]{0:T(1024)S(1)} %bitcast.66, f32[128]{0:T(128)S(1)} %get-tuple-element.74, f32[128]{0:T(128)S(1)} %get-tuple-element.75), kind=kLoop, calls=%fused_computation | loop fusion | flops 25165568 | bytes 264192 | tf_op jit(solution)/shard_map/reduce_sum | solution.py:88
  90.5 0.0 copy-done.2
  90.5 0.3 add_tanh_fusion
  90.8 1.0 fusion.48
  91.8 0.2 subtract_multiply_fusion.3
  92.0 1.1 fusion.52
  93.0 0.2 subtract_multiply_fusion.2
  93.2 1.0 fusion.56
  94.3 0.2 subtract_multiply_fusion.1
  94.5 1.1 fusion.60
  95.5 0.0 copy-start.7
  95.5 0.2 multiply_reduce_fusion
  95.8 0.4 copy-done.7
  96.2 0.4 fusion.102
  96.6 1.5 fusion.32
  98.2 1.7 fusion.47
  99.9 0.4 fusion.97
  100.3 1.5 fusion.35
  101.8 1.5 fusion.46
  103.3 0.4 fusion.96
  103.7 1.5 fusion.38
  105.2 1.5 fusion.45
  106.6 0.4 fusion.95
  107.0 1.5 fusion.41
  108.5 2.5 pad_maximum_fusion
  111.0 0.0 copy-start.3
  111.0 0.0 copy-start.5
  111.0 0.0 copy-start.4
  111.0 0.0 all-reduce.4.cloned.1.call-update
  111.0 0.6 copy-done.3
  111.7 0.0 copy-done.5
  111.7 0.0 copy-done.4
  111.7 0.0 copy-done.6
  111.7 2.7 fusion.44
  114.4 0.6 add_reduce_fusion.1
  115.0 73.2 %all-reduce.1 = (f32[2,512]{1,0:T(2,128)}, f32[512]{0:T(512)}) all-reduce(f32[2,512]{1,0:T(2,128)S(1)} %pad_maximum_fusion.18, f32[512]{0:T(512)S(1)} %get-tuple-element.43), channel_id=1, replica_groups=mesh['wide'=64,'narrow'=4] {'wide','narrow'}, use_global_device_ids=true, to_apply=%region_7.8 | all-reduce | flops 1536 | bytes 12288 | tf_op jit(solution)/shard_map/psum | solution.py:115
  188.3 188.8 %all-reduce.4.cloned.1.call-done = f32[4,512,512]{2,1,0:T(8,128)} async-done(((f32[4,512,512]{2,1,0:T(8,128)}), f32[4,512,512]{2,1,0:T(8,128)}) %all-reduce.4.cloned.1.call-update) | async-done | bytes 4194320 | tf_op jit(solution)/shard_map/psum | solution.py:115
  377.1 4.6 %copy.19 = f32[4,512,512]{2,1,0:T(8,128)} copy(f32[4,512,512]{2,1,0:T(8,128)} %all-reduce.4.cloned.1.call-done) | data formatting | bytes 8388608
  (12 shorter events, 0.1 us)
Async XLA Ops:
  7.2 369.9 %all-reduce.4.cloned.1.call-start = ((), (), s32[]{:S(2)}) async-start(), calls=%async_computation | async-start | bytes 8388608 | tf_op jit(solution)/shard_map/psum | solution.py:115
  13.8 2.5 copy-start
  17.0 0.8 copy-start.8
  17.0 0.8 copy-start.9
  17.0 0.8 copy-start.1
  17.8 72.7 %copy-start.2 = (f32[512]{0:T(512)S(1)}, f32[512]{0:T(512)}, u32[]{:S(2)}) copy-start(f32[512]{0:T(512)} %param.20) | copy-start | bytes 6148
  95.5 0.7 copy-start.7
  111.0 0.7 copy-start.3
  111.0 0.7 copy-start.5
  111.0 0.7 copy-start.4
  111.0 0.7 copy-start.6
Sparse Core Ops, SparseCore 0:
  111.1 265.9 all-reduce.3
where the time goes:
time: 389 us
  waiting for transfers between devices  189 us (49%)
  blocking collectives  141 us (36%)
  matrix products  22.6 us (6%)
  between operations  14.4 us (4%)
  other arithmetic  11.6 us (3%)
  local copies, waits for them, and re-layouts  10.3 us (3%)
    psum x1, waiting for transfers between devices, local(): first, hidden, last = lax.psum((first, hidden, last), BOTH)  189 us
    psum x1, blocking collectives, local(): first, hidden, last = lax.psum((first, hidden, last), BOTH)  73.2 us
    all_gather x1, blocking collectives, local(): everyone = lax.all_gather(mine, BOTH)  67.6 us
    dot_general x8, matrix products, forward(): jnp.dot(jnp.concatenate([hidden, tangent], 0), w_hidden[level], precision...  9.35 us
  transfers between devices with their start and end apart: 1, of which 1 were waited for; matrix products, arithmetic and copies ran while one was open for 1% of the time, Pallas kernels for 0%

commit v1 on v0

--- a/solution.py
+++ b/solution.py
@@ -112,7 +112,7 @@
         w_first,
         w_hidden,
     )
-    first, hidden, last = lax.psum((first, hidden, last), BOTH)
+    first, hidden, last = lax.psum(lax.psum((first, hidden, last), "narrow"), "wide")
     return (integral, first, hidden, last)
 
 

time: 389 us -> 417 us (1.072)
  blocking collectives: 141 us -> 207 us
  waiting for transfers between devices: 189 us -> 150 us
    psum x1 -> x2, blocking collectives: 73.2 us -> 139 us  [the longest x1 130 us: local(): lax.psum(lax.psum((first, hidden, last), 'narrow'), 'wide')]
    psum x1 -> x2, waiting for transfers between devices: 189 us -> 150 us  [the longest x1 92.5 us: local(): lax.psum((first, hidden, last), 'narrow')]
  transfers between devices with their start and end apart: 1 -> 2, of which waited for: 1 -> 2; matrix products, arithmetic and copies ran while one was open for 1% -> 1% of each run, Pallas kernels for 0% -> 0%
where the time goes in v1:
time: 417 us; the launch traced here: 416 us
  blocking collectives  207 us (50%)
  waiting for transfers between devices  150 us (36%)
  matrix products  22.6 us (5%)
  between operations  14.4 us (3%)
  other arithmetic  11.6 us (3%)
  local copies, waits for them, and re-layouts  10.3 us (2%)
    psum x1, blocking collectives, local(): lax.psum(lax.psum((first, hidden, last), 'narrow'), 'wide')  130 us
    psum x1, waiting for transfers between devices, local(): lax.psum((first, hidden, last), 'narrow')  92.5 us
    all_gather x1, blocking collectives, local(): everyone = lax.all_gather(mine, BOTH)  67.6 us
    psum x1, waiting for transfers between devices, local(): lax.psum(lax.psum((first, hidden, last), 'narrow'), 'wide')  57.9 us
    psum x1, blocking collectives, local(): lax.psum((first, hidden, last), 'narrow')  9.47 us
    dot_general x8, matrix products, forward(): jnp.dot(jnp.concatenate([hidden, tangent], 0), w_hidden[level], precision...  9.35 us
  transfers between devices with their start and end apart: 2, of which 2 were waited for; matrix products, arithmetic and copies ran while one was open for 1% of the time, Pallas kernels for 0%

profile of v1, /device:TPU:2, one launch (start us, length us, event | category | flops | bytes accessed | tf_op | source)
XLA Modules:
  0.0 416.1 jit_solution(13161066144697224354)
XLA Ops:
  7.2 0.0 all-reduce.6.cloned.1.call-start
  7.2 0.8 fusion.155
  8.0 0.8 fusion.156
  8.7 0.8 fusion.154
  9.5 0.9 fusion.153
  10.4 0.8 slice_bitcast_fusion.1
  11.2 0.8 add_tanh_fusion.1
  12.0 1.8 fusion.78
  13.9 0.0 copy-start
  13.9 0.1 subtract_multiply_fusion.7
  13.9 2.0 fusion.74
  16.0 0.1 subtract_multiply_fusion.6
  16.0 0.3 copy-done
  16.4 0.7 fusion.70
  17.0 0.0 copy-start.8
  17.0 0.0 copy-start.9
  17.0 0.0 copy-start.1
  17.1 0.1 subtract_multiply_fusion.5
  17.1 0.6 fusion.66
  17.8 0.0 copy-done.8
  17.8 0.0 copy-done.9
  17.8 0.0 copy-start.2
  17.8 0.0 copy-done.1
  17.8 0.2 multiply_reduce_fusion.2
  18.0 67.6 %all-gather.1 = f32[256,2,128]{2,1,0:T(2,128)S(1)} all-gather(f32[1,2,128]{2,1,0:T(2,128)S(1)} %maximum_bitcast_fusion), channel_id=2, replica_groups=mesh['wide'=64,'narrow'=4] {'wide','narrow'}, dimensions={0}, use_global_device_ids=true | all-gather | bytes 263168 | tf_op jit(solution)/shard_map/all_gather | solution.py:83
  85.6 0.2 fusion.152
  85.8 4.7 %select_reduce_fusion = (f32[128]{0:T(128)S(1)}, f32[128]{0:T(128)}) fusion(f32[32768]{0:T(1024)S(1)} %bitcast.67, f32[32768]{0:T(1024)S(1)} %bitcast.66, f32[128]{0:T(128)S(1)} %get-tuple-element.76, f32[128]{0:T(128)S(1)} %get-tuple-element.77), kind=kLoop, calls=%fused_computation | loop fusion | flops 25165568 | bytes 264192 | tf_op jit(solution)/shard_map/reduce_sum | solution.py:88
  90.5 0.3 add_tanh_fusion
  90.8 1.0 fusion.48
  91.8 0.2 subtract_multiply_fusion.3
  92.0 1.1 fusion.52
  93.1 0.2 subtract_multiply_fusion.2
  93.2 1.1 fusion.56
  94.3 0.2 subtract_multiply_fusion.1
  94.5 1.0 fusion.60
  95.5 0.0 copy-start.7
  95.5 0.2 multiply_reduce_fusion
  95.8 0.4 copy-done.7
  96.2 0.4 fusion.102
  96.7 1.5 fusion.32
  98.2 1.7 fusion.47
  99.9 0.4 fusion.97
  100.3 1.5 fusion.35
  101.8 1.5 fusion.46
  103.3 0.4 fusion.96
  103.7 1.5 fusion.38
  105.2 1.5 fusion.45
  106.6 0.4 fusion.95
  107.0 1.5 fusion.41
  108.5 2.5 pad_maximum_fusion
  111.0 0.0 all-reduce.6.cloned.1.call-update
  111.0 0.0 all-reduce.8.cloned.1.call-start
  111.1 92.5 %all-reduce.6.cloned.1.call-done = f32[4,512,512]{2,1,0:T(8,128)} async-done(((f32[4,512,512]{2,1,0:T(8,128)}), f32[4,512,512]{2,1,0:T(8,128)}) %all-reduce.6.cloned.1.call-update) | async-done | bytes 4194320 | tf_op jit(solution)/shard_map/psum | solution.py:115
  203.5 0.0 all-reduce.8.cloned.1.call-update
  203.6 0.6 copy-done.3
  204.2 0.0 copy-done.5
  204.2 0.0 copy-done.4
  204.2 0.0 copy-done.6
  204.3 2.7 fusion.44
  207.0 0.6 add_reduce_fusion.1
  207.6 9.5 %all-reduce.2 = (f32[2,512]{1,0:T(2,128)S(1)}, f32[512]{0:T(512)S(1)}) all-reduce(f32[2,512]{1,0:T(2,128)S(1)} %pad_maximum_fusion.18, f32[512]{0:T(512)S(1)} %get-tuple-element.45), channel_id=1, replica_groups=mesh['wide'=64,'narrow'=4] {'narrow'}, use_global_device_ids=true, to_apply=%region_7.8 | all-reduce | flops 1536 | bytes 12288 | tf_op jit(solution)/shard_map/psum | solution.py:115
  217.1 129.6 %all-reduce.1 = (f32[2,512]{1,0:T(2,128)}, f32[512]{0:T(512)}) all-reduce(f32[2,512]{1,0:T(2,128)S(1)} %get-tuple-element.16, f32[512]{0:T(512)S(1)} %get-tuple-element.17), channel_id=1, replica_groups=mesh['wide'=64,'narrow'=4] {'wide'}, use_global_device_ids=true, to_apply=%region_8.9 | all-reduce | flops 1536 | bytes 12288 | tf_op jit(solution)/shard_map/psum | solution.py:115
  346.6 57.9 %all-reduce.8.cloned.1.call-done = f32[4,512,512]{2,1,0:T(8,128)} async-done(((f32[4,512,512]{2,1,0:T(8,128)}), f32[4,512,512]{2,1,0:T(8,128)}) %all-reduce.8.cloned.1.call-update) | async-done | bytes 4194320 | tf_op jit(solution)/shard_map/psum | solution.py:115
  404.6 4.6 %copy.20 = f32[4,512,512]{2,1,0:T(8,128)} copy(f32[4,512,512]{2,1,0:T(8,128)} %all-reduce.8.cloned.1.call-done) | data formatting | bytes 8388608
  (16 shorter events, 0.1 us)
Async XLA Ops:
  7.2 196.4 %all-reduce.6.cloned.1.call-start = ((), (), s32[]{:S(2)}) async-start(), calls=%async_computation | async-start | bytes 8388608 | tf_op jit(solution)/shard_map/psum | solution.py:115
  13.9 2.5 copy-start
  17.0 0.8 copy-start.8
  17.0 0.8 copy-start.9
  17.0 0.8 copy-start.1
  17.8 72.7 %copy-start.2 = (f32[512]{0:T(512)S(1)}, f32[512]{0:T(512)}, u32[]{:S(2)}) copy-start(f32[512]{0:T(512)} %param.20) | copy-start | bytes 6148
  95.5 0.7 copy-start.7
  111.0 293.6 %all-reduce.8.cloned.1.call-start = ((), (), s32[]{:S(2)}) async-start(), calls=%async_computation.1 | async-start | bytes 8388608 | tf_op jit(solution)/shard_map/psum | solution.py:115
  203.5 0.7 copy-start.3
  203.5 0.7 copy-start.5
  203.5 0.7 copy-start.4
  203.5 0.7 copy-start.6
Sparse Core Ops, SparseCore 0:
  111.1 92.3 all-reduce.5
  207.1 197.4 all-reduce.7
